TPU v7x, 16 devices: a whole 2x2x2 slice. The times are simulated.
16 devices in a mesh: data: 16 (over z, y, x, core).
Axes of the slice: x: 2, y: 2, z: 2, core: 2. Of those that a mesh axis runs over, the one named last changes fastest.
Arguments:
- tokens: bfloat16 [512, 1600], P('data')
- labels: int32 [8, 512], P(None, 'data')
- w_one: bfloat16 [1600, 6400], replicated
- w_two: bfloat16 [6400, 1600], replicated
- adapter_a: bfloat16 [1600, 16], replicated
- adapter_b: bfloat16 [16, 6400], replicated
- task_heads: bfloat16 [8, 1600, 2], replicated
Outputs:
- output 1: float32 [8], replicated
- output 2: float32 [1600, 16], P('data')
- output 3: float32 [16, 6400], P(None, 'data')
All inputs are finite; a program needn't handle non-finite values.
Results may differ from a plain program's by a relative error of at most 0.00184.
Values are sent between devices in bfloat16 or wider.
A program may use at most 1 GiB of HBM per device.

v0:
```python
import jax
import jax.numpy as jnp
from jax import lax
from jax.sharding import PartitionSpec as P

EG_STEPS = 20


def weight_solver(gram_mat):
    num_tasks = gram_mat.shape[0]
    eg_scale = jnp.trace(gram_mat) / num_tasks

    def eg_step(step_idx, weights):
        weights = weights * jnp.exp(-jnp.sum(gram_mat * weights[None, :], axis=1) / eg_scale)
        return weights / jnp.sum(weights)

    return lax.fori_loop(0, EG_STEPS, eg_step, jnp.full((num_tasks,), 1.0 / num_tasks, jnp.float32))


def task_grads(tokens, labels, w_one, w_two, adapter_a, adapter_b, task_heads):
    num_classes = task_heads.shape[2]
    low_rank = jnp.dot(tokens, adapter_a, preferred_element_type=jnp.float32).astype(jnp.bfloat16)
    pre_act = jnp.dot(tokens, w_one, preferred_element_type=jnp.float32) + jnp.dot(low_rank, adapter_b, preferred_element_type=jnp.float32)
    gelu_out, gelu_slope = jax.jvp(jax.nn.gelu, (pre_act,), (jnp.ones_like(pre_act),))
    hidden = gelu_out.astype(jnp.bfloat16)
    trunk_out = (tokens.astype(jnp.float32) + jnp.dot(hidden, w_two, preferred_element_type=jnp.float32)).astype(jnp.bfloat16)
    logits = jnp.einsum("bd,tdc->tbc", trunk_out, task_heads, preferred_element_type=jnp.float32)
    task_probs = jax.nn.softmax(logits, axis=-1)
    onehot = (labels[:, :, None] == jnp.arange(num_classes)[None, None, :]).astype(jnp.float32)
    logit_err = (task_probs - onehot).astype(jnp.bfloat16)
    d_trunk = jnp.einsum("tbc,tdc->tbd", logit_err, task_heads, preferred_element_type=jnp.float32).astype(jnp.bfloat16)
    d_hidden = jnp.einsum("tbd,fd->tbf", d_trunk, w_two, preferred_element_type=jnp.float32)
    d_pre = (d_hidden * gelu_slope[None]).astype(jnp.bfloat16)
    part_b = jnp.einsum("cs,ucg->usg", low_rank, d_pre, preferred_element_type=jnp.float32)
    d_low = jnp.einsum("tbf,rf->tbr", d_pre, adapter_b, preferred_element_type=jnp.float32).astype(jnp.bfloat16)
    part_a = jnp.einsum("bd,tbr->tdr", tokens, d_low, preferred_element_type=jnp.float32)
    return part_a, part_b


def solution(mesh):
    num_dev = mesh.shape["data"]

    def device_step(tokens, labels, w_one, w_two, adapter_a, adapter_b, task_heads):
        batch_total = tokens.shape[0] * num_dev
        part_a, part_b = task_grads(tokens, labels, w_one, w_two, adapter_a, adapter_b, task_heads)
        shard_a = lax.psum_scatter(part_a, "data", scatter_dimension=1, tiled=True) / batch_total
        shard_b = lax.psum_scatter(part_b, "data", scatter_dimension=2, tiled=True) / batch_total
        gram_part = jnp.einsum("tdr,sdr->ts", shard_a, shard_a, precision=lax.Precision.HIGHEST) + jnp.einsum("usg,tsg->ut", shard_b, shard_b, precision=lax.Precision.HIGHEST)
        gram_mat = lax.psum(gram_part, "data")
        task_weights = weight_solver(gram_mat)
        comb_a = jnp.sum(task_weights[:, None, None] * shard_a, axis=0)
        comb_b = jnp.sum(task_weights[:, None, None] * shard_b, axis=0)
        return task_weights, comb_a, comb_b

    return jax.shard_map(device_step, mesh=mesh, in_specs=(P("data", None), P(None, "data"), P(), P(), P(), P(), P()), out_specs=(P(), P("data", None), P(None, "data")), check_vma=False)
```

profile of v0, /device:TPU:0, one launch (start us, length us, event | category | flops | bytes accessed | tf_op | source)
XLA Modules:
  0.0 251.8 jit_solution(5532037381682938900)
XLA Ops:
  7.2 1.1 convolution_convert_fusion.2
  8.3 8.8 %fusion.52 = f32[32,6400]{1,0:T(8,128)S(1)} fusion(bf16[32,1600]{1,0:T(8,128)(2,1)} %param.9, bf16[1600,6400]{1,0:T(8,128)(2,1)} %param.11), kind=kOutput, calls=%fused_computation.64 | convolution fusion | flops 655360000 | bytes 21401600 | tf_op jit(solution)/shard_map/dot_general | solution.py:23
  17.1 1.6 fusion.22
  18.7 13.0 %fusion.51 = (f32[8,32]{1,0:T(8,128)S(1)}, f32[8,32,2]{1,0,2:T(8,128)S(1)}) fusion(bf16[8,1600,2]{1,2,0:T(2,128)(2,1)S(1)} %copy-done.4, bf16[6400,1600]{0,1:T(8,128)(2,1)} %param.12, f32[32,6400]{1,0:T(8,128)S(1)} %get-tuple-element.52, bf16[32,1600]{1,0:T(8,128)(2,1)S(1)} %copy-done.3), kind=kOutput, calls=%fused_computation.63 | convolution fusion | flops 658995456 | bytes 21455872 | tf_op jit(solution)/shard_map/bd,tdc->tbc/dot_general | solution.py:27
  31.7 11.3 %fusion.5 = bf16[8,32,6400]{2,1,0:T(8,128)(2,1)S(1)} fusion(bf16[6400,1600]{0,1:T(8,128)(2,1)} %param.12, f32[32,6400]{1,0:T(8,128)} %get-tuple-element.51, bf16[8,1600,2]{1,2,0:T(2,128)(2,1)S(1)} %copy-done.4, bf16[8,32,2]{1,0,2:T(8,128)(2,1)S(1)} %subtract_convert_fusion), kind=kOutput, calls=%fused_computation.7 | convolution fusion | flops 5248204800 | bytes 24628224 | tf_op jit(solution)/shard_map/tbd,fd->tbf/dot_general | solution.py:32
  43.0 4.4 %convolution_bitcast_fusion.1 = f32[8,1600,16]{1,2,0:T(8,128)} fusion(bf16[8,32,6400]{2,1,0:T(8,128)(2,1)S(1)} %fusion.5, bf16[16,6400]{1,0:T(8,128)(2,1)S(1)} %copy-done, bf16[32,1600]{1,0:T(8,128)(2,1)} %param.9), kind=kOutput, calls=%fused_computation.11 | convolution fusion | flops 65540096 | bytes 4403200 | tf_op jit(solution)/shard_map/bd,tbr->tdr/dot_general | solution.py:36
  47.4 0.2 reduce-scatter.5.cloned.1.call-start
  47.6 2.5 convolution_bitcast_fusion
  50.1 12.3 %copy.23 = f32[8,16,6400]{1,0,2:T(8,128)} copy(f32[8,16,6400]{2,1,0:T(8,128)S(1)} %convolution_bitcast_fusion) | data formatting | bytes 6553600
  62.4 17.0 %reshape.21 = f32[6400,128]{1,0:T(8,128)} reshape(f32[6400,8,16]{2,1,0:T(8,128)} %bitcast.53) | data formatting | bytes 6553600
  79.4 37.7 %all-reduce.3.cloned.1.call-done = f32[8,1600,16]{1,2,0:T(8,128)} async-done(((f32[8,1600,16]{1,2,0:T(8,128)}), f32[8,1600,16]{1,2,0:T(8,128)}) %all-reduce.3.cloned.1.call-update) | async-done | bytes 819216
  117.1 1.0 dynamic-slice_multiply_fusion
  118.1 0.2 convolution_bitcast_fusion.2
  118.3 61.0 %reduce-scatter.5.cloned.1.call-done = f32[400,128]{1,0:T(8,128)} async-done(((f32[6400,128]{1,0:T(8,128)}), f32[400,128]{1,0:T(8,128)}) %reduce-scatter.5.cloned.1.call-update) | async-done | bytes 204816
  179.3 1.4 reshape.22
  180.7 0.6 copy.24
  181.4 0.7 fusion.12
  182.1 30.9 %psum.7 = f32[8,8]{1,0:T(8,128)S(1)} all-reduce(f32[8,8]{1,0:T(8,128)S(1)} %fusion.12), channel_id=1, replica_groups=mesh['data'=16] {'data'}, use_global_device_ids=true, to_apply=%region_4.0 | all-reduce | flops 64 | bytes 512 | tf_op jit(solution)/shard_map/psum | solution.py:49
  213.0 0.6 select_reduce_fusion
  214.3 28.4 %while.11 = (s32[]{:T(128)}, f32[8]{0:T(128)S(1)}, f32[8,8]{1,0:T(8,128)S(1)}, f32[]{:T(128)}, s32[]{:T(128)}, /*index=5*/s32[]{:T(128)}) while((s32[]{:T(128)}, f32[8]{0:T(128)S(1)}, f32[8,8]{1,0:T(8,128)S(1)}, f32[]{:T(128)}, s32[]{:T(128)}, /*index=5*/s32[]{:T(128)}) %tuple.31), condition=%wide.region_9.10_spmd.clone, body=%wide.region_6.9_spmd.clone.sunk | while | flops 178 | bytes 636 | solution.py:17
  214.4 0.6 fusion.64
  215.0 0.6 broadcast_divide_fusion.2
  215.8 0.6 fusion.64
  216.4 0.6 broadcast_divide_fusion.2
  217.2 0.6 fusion.64
  217.9 0.6 broadcast_divide_fusion.2
  218.7 0.6 fusion.64
  219.3 0.6 broadcast_divide_fusion.2
  220.1 0.6 fusion.64
  220.7 0.6 broadcast_divide_fusion.2
  221.5 0.6 fusion.64
  222.1 0.6 broadcast_divide_fusion.2
  222.9 0.6 fusion.64
  223.5 0.6 broadcast_divide_fusion.2
  224.3 0.6 fusion.64
  224.9 0.6 broadcast_divide_fusion.2
  225.7 0.6 fusion.64
  226.4 0.6 broadcast_divide_fusion.2
  227.2 0.6 fusion.64
  227.8 0.6 broadcast_divide_fusion.2
  228.6 0.6 fusion.64
  229.2 0.6 broadcast_divide_fusion.2
  229.9 0.1 multiply_reduce_fusion.4
  230.0 0.6 fusion.64
  230.6 0.6 broadcast_divide_fusion.2
  231.3 0.1 multiply_reduce_fusion.4
  231.4 0.6 fusion.64
  232.0 0.6 broadcast_divide_fusion.2
  232.8 0.6 fusion.64
  233.5 0.6 broadcast_divide_fusion.2
  234.3 0.6 fusion.64
  234.9 0.6 broadcast_divide_fusion.2
  235.7 0.6 fusion.64
  236.3 0.6 broadcast_divide_fusion.2
  237.1 0.6 fusion.64
  237.7 0.6 broadcast_divide_fusion.2
  238.5 0.6 fusion.64
  239.1 0.6 broadcast_divide_fusion.2
  239.9 0.6 fusion.64
  240.5 0.6 broadcast_divide_fusion.2
  241.3 0.6 fusion.64
  242.0 0.6 broadcast_divide_fusion.2
  242.7 0.7 multiply_reduce_fusion.1
  243.4 1.6 multiply_reduce_fusion.2
  (60 shorter events, 2.4 us)
Async XLA Ops:
  7.2 9.9 %copy-start = (bf16[16,6400]{1,0:T(8,128)(2,1)S(1)}, bf16[16,6400]{1,0:T(8,128)(2,1)}, u32[]{:S(2)}) copy-start(bf16[16,6400]{1,0:T(8,128)(2,1)} %param.14) | copy-start | bytes 614404
  7.2 109.9 %all-reduce.3.cloned.1.call-start = ((), (), s32[]{:S(2)}) async-start(), calls=%async_computation.2 | async-start | bytes 1703936
  8.3 10.4 %copy-start.3 = (bf16[32,1600]{1,0:T(8,128)(2,1)S(1)}, bf16[32,1600]{1,0:T(8,128)(2,1)}, u32[]{:S(2)}) copy-start(bf16[32,1600]{1,0:T(8,128)(2,1)} %param.9) | copy-start | bytes 307204
  8.3 10.4 %copy-start.4 = (bf16[8,1600,2]{1,2,0:T(2,128)(2,1)S(1)}, bf16[8,1600,2]{1,2,0:T(2,128)(2,1)}, u32[]{:S(2)}) copy-start(bf16[8,1600,2]{1,2,0:T(2,128)(2,1)} %param.15) | copy-start | bytes 153604
  18.7 13.0 %copy-start.6 = (s32[8,32]{1,0:T(8,128)S(1)}, s32[8,32]{1,0:T(8,128)}, u32[]{:S(2)}) copy-start(s32[8,32]{1,0:T(8,128)} %param.10) | copy-start | bytes 3076
  43.0 4.4 %copy-start.2 = (bf16[8,32,6400]{2,1,0:T(8,128)(2,1)}, bf16[8,32,6400]{2,1,0:T(8,128)(2,1)S(1)}, u32[]{:S(2)}) copy-start(bf16[8,32,6400]{2,1,0:T(8,128)(2,1)S(1)} %fusion.5) | copy-start | bytes 9830404
  47.4 131.9 %reduce-scatter.5.cloned.1.call-start = ((), (), s32[]{:S(2)}) async-start(), calls=%async_computation.1 | async-start | bytes 3481600
  62.4 182.5 %copy-start.1 = (bf16[16,6400]{1,0:T(8,128)(2,1)S(1)}, bf16[16,6400]{1,0:T(8,128)(2,1)}, u32[]{:S(2)}) copy-start(bf16[16,6400]{1,0:T(8,128)(2,1)} %param.14) | copy-start | bytes 614404
  242.6 2.3 copy-start.5
Sparse Core Ops, SparseCore 0:
  47.5 69.5 all-reduce.2
  119.4 59.8 reduce-scatter.4
where the time goes:
time: 253 us; the launch traced here: 252 us
  waiting for transfers between devices  98.7 us (39%)
  matrix products  43.4 us (17%)
  other arithmetic  31.7 us (13%)
  local copies, waits for them, and re-layouts  31.3 us (12%)
  blocking collectives  30.9 us (12%)
  between operations  14.9 us (6%)
    unnamed x4, waiting for transfers between devices  98.7 us
    unnamed x18, local copies, waits for them, and re-layouts  31.3 us
    psum x1, blocking collectives, device_step(): gram_mat = lax.psum(gram_part, 'data')  30.9 us
    dot_general x1, matrix products, task_grads(): jnp.einsum('bd,tdc->tbc', trunk_out, task_heads, preferred_element_type=j...  13 us
    div x20, other arithmetic, eg_step(): return weights / jnp.sum(weights)  13 us
    reduce_sum x20, other arithmetic, eg_step(): return weights / jnp.sum(weights)  12.4 us
    dot_general x1, matrix products, task_grads(): jnp.einsum('tbd,fd->tbf', d_trunk, w_two, preferred_element_type=jnp.floa...  11.3 us
    dot_general x1, matrix products, task_grads(): jnp.dot(tokens, w_one, preferred_element_type=jnp.float32)  8.76 us
  transfers between devices with their start and end apart: 2, of which 2 were waited for; matrix products, arithmetic and copies ran while one was open for 13% of the time, Pallas kernels for 0%

commit v1 on v0

v1 whole, which is shorter than its diff:
```python
import jax
import jax.numpy as jnp
from jax import lax
from jax.experimental import pallas as pl
from jax.experimental.pallas import tpu as pltpu
from jax.sharding import PartitionSpec as P

EG_STEPS = 20
F32 = jnp.float32
BF16 = jnp.bfloat16
MESH = pl.DeviceIdType.MESH

N_CHIP, N_CORE = 8, 2
TOK = 32
D, FF, R, T, C = 1600, 6400, 16, 8, 2
DP = 1664
HALF = FF // N_CORE
BLK = FF // N_CHIP
OWN = BLK // N_CORE
WIN = 896
OWIN = 512
W1_CHUNKS = ((0, 768), (768, 768), (1536, 768), (2304, 896))
W2_CHUNKS = ((0, 512), (512, 512), (1024, 512), (1536, 128))
ORDER = (1, 3, 5, 7, 6, 2, 4, 0)
GELU_C = 0.7978845608028654
N_TILE = 256


def nt(a, b):
    return lax.dot_general(a, b, (((1,), (1,)), ((), ())), preferred_element_type=F32)


def tn(a, b):
    return lax.dot_general(a, b, (((0,), (0,)), ((), ())), preferred_element_type=F32)


def nn(a, b):
    return jnp.dot(a, b, preferred_element_type=F32)


def gelu(p):
    th = jnp.tanh(GELU_C * (p + 0.044715 * (p * p * p)))
    return p * (0.5 * (1.0 + th))


def gelu_slope(p):
    p2 = p * p
    th = jnp.tanh(GELU_C * (p + 0.044715 * (p2 * p)))
    return 0.5 * (1.0 + th) + (0.5 * p * (1.0 - th * th)) * (GELU_C * (1.0 + 0.134145 * p2))


def iota(shape, dim):
    return lax.broadcasted_iota(jnp.int32, shape, dim)


def gram_parts(blocks):
    acc = [None] * 5
    for v in blocks:
        for k in range(5):
            w = v * (v if k == 0 else pltpu.roll(v, k, 0))
            w = sum(w[:, i : i + 128] for i in range(0, w.shape[1], 128))
            acc[k] = w if acc[k] is None else acc[k] + w
    return acc


def kernel(
    x_hbm, lab_hbm, w1_hbm, w2_hbm, at_hbm, bm_hbm, hd_hbm,
    alpha_out, ga_out, gb_out,
    w1h, w2h, w1w, w2w, bmh, bmw, at, hd, lab, xp, xall, hbuf, hs, ha, hb, bmt, urep, g,
    zown, zsend, zrecv, eown, eall, dz, dp, dsend, drecv, duown, duall, gb, gbrecv, mown, mall, ga,
    lsem, xs, xr, ps, pr, zs, zr, es, er, ds_, dr, bs, br, ns, nr, ms, mr, gs, gr,
):
    me = lax.axis_index("data")
    chip, core = me // N_CORE, me % N_CORE
    cx, cy, cz = chip % 2, (chip // 2) % 2, chip // 4
    mate = 1 - core

    def peer(m):
        px = 1 - cx if m & 1 else cx
        py = 1 - cy if m & 2 else cy
        pz = 1 - cz if m & 4 else cz
        return 4 * pz + 2 * py + px

    def rcopy(src, dst, ssem, rsem, chip_to, core_to):
        return pltpu.make_async_remote_copy(
            src_ref=src, dst_ref=dst, send_sem=ssem, recv_sem=rsem,
            device_id=(N_CORE * chip_to + core_to,), device_id_type=MESH,
        )

    n_sem = [0]

    def load(src, dst):
        c = pltpu.make_async_copy(src, dst, lsem.at[n_sem[0]])
        n_sem[0] += 1
        c.start()
        return c

    half0 = pl.multiple_of(core * HALF, 128)
    tile0 = (BLK * chip) // 128
    win0 = pl.multiple_of(tile0 * 128, 128)
    off = BLK * chip - win0
    c_x = load(x_hbm, xp.at[pl.ds(0, TOK)])
    c_at = load(at_hbm, at)
    c_hd = load(hd_hbm, hd)
    c_lab = load(lab_hbm, lab)
    c_bmh = load(bm_hbm.at[:, pl.ds(half0, HALF)], bmh)
    c_w1 = [load(w1_hbm.at[:, pl.ds(pl.multiple_of(half0 + a, 128), n)], w1h.at[:, pl.ds(a, n)]) for a, n in W1_CHUNKS]
    c_w2 = [
        load(w2_hbm.at[pl.ds(a, min(n, D - a)), pl.ds(half0, HALF)], w2h.at[pl.ds(a, min(n, D - a))]) for a, n in W2_CHUNKS
    ]
    c_bmw = load(bm_hbm.at[:, pl.ds(win0, WIN)], bmw)
    c_w1w = load(w1_hbm.at[:, pl.ds(win0, WIN)], w1w)
    c_w2w = load(w2_hbm.at[:, pl.ds(win0, WIN)], w2w)

    barrier = pltpu.get_barrier_semaphore()
    for m in range(N_CHIP):
        for other in range(N_CORE):
            if m or other:
                pl.semaphore_signal(
                    barrier, inc=1, device_id=(N_CORE * peer(m) + (mate if other else core),), device_id_type=MESH
                )

    hbuf[...] = jnp.zeros_like(hbuf)
    w2h[pl.ds(D, DP - D), :] = jnp.zeros((DP - D, HALF), BF16)
    eown[...] = jnp.zeros_like(eown)
    row_of_r = (iota((R, R * T), 1) // T == iota((R, R * T), 0)).astype(F32).astype(BF16)
    c_hd.wait()
    for t in range(T):
        v = hd[t].astype(F32)
        for c in range(C):
            hs[pl.ds(c * T + t, 1), :] = v[c : c + 1]
    ha[...] = hs[...].astype(BF16)
    hb[...] = jnp.concatenate([hs[T:, :], hs[:T, :]], axis=0).astype(BF16)
    c_lab.wait()
    lab_f = lab[...].astype(F32)
    eye = (iota((TOK, TOK), 0) == iota((TOK, TOK), 1)).astype(F32).astype(BF16)
    lab_t = nt(eye, jnp.concatenate([lab_f, lab_f], axis=0).astype(BF16))
    onehot = (lab_t == (iota((TOK, C * T), 1) // T).astype(F32)).astype(F32)
    c_x.wait()
    my_row = pl.multiple_of(core * (N_CHIP * TOK) + chip * TOK, TOK)
    xall[pl.ds(my_row, TOK), :] = xp[pl.ds(0, TOK), :]

    pl.semaphore_wait(barrier, N_CHIP * N_CORE - 1)

    k_xp = rcopy(xp.at[pl.ds(0, TOK)], xp.at[pl.ds(TOK, TOK)], ps, pr, chip, mate)
    k_xp.start()
    k_x = {}
    for m in (1, 2, 4, 3, 5, 6, 7):
        k_x[m] = rcopy(xp.at[pl.ds(0, TOK)], xall.at[pl.ds(my_row, TOK)], xs.at[m], xr.at[m], peer(m), core)
        k_x[m].start()

    c_at.wait()
    k_xp.wait_recv()
    x2 = xp[...]
    u2 = nt(x2, at[...]).astype(BF16)
    c_bmh.wait()
    for (a, n), cp in zip(W1_CHUNKS, c_w1):
        cp.wait()
        pre = nn(x2, w1h[:, a : a + n]) + nn(u2, bmh[:, a : a + n])
        hbuf[pl.ds(0, 2 * TOK), a : a + n] = gelu(pre).astype(BF16)
    k_z = []
    for i, ((a, n), cp) in enumerate(zip(W2_CHUNKS, c_w2)):
        cp.wait()
        zt = nt(w2h[pl.ds(a, n), :], hbuf[...])
        z = jnp.transpose(zt)
        zown[:, a : a + n] = z[:TOK]
        zsend[:, a : a + n] = z[TOK : 2 * TOK]
        k_z.append(rcopy(zsend.at[:, pl.ds(a, n)], zrecv.at[:, pl.ds(a, n)], zs.at[i], zr.at[i], chip, mate))
        k_z[-1].start()
    for k in k_z:
        k.wait_recv()
    xf = xp[pl.ds(0, TOK), :].astype(F32)
    zb = (xf + (zown[:, :D] + zrecv[:, :D])).astype(BF16)
    la, lb = nt(zb, ha[...]), nt(zb, hb[...])
    top = jnp.maximum(la, lb)
    ea, eb = jnp.exp(la - top), jnp.exp(lb - top)
    err = (ea / (ea + eb) - onehot).astype(BF16)
    eown[:, : C * T] = err
    my_slot = pl.multiple_of(chip * TOK, TOK)
    eall[pl.ds(my_slot, TOK), :] = eown[...]
    k_e = {}
    for m in (1, 2, 4, 3, 5, 6, 7):
        k_e[m] = rcopy(eown, eall.at[pl.ds(my_slot, TOK)], es.at[m], er.at[m], peer(m), core)
        k_e[m].start()

    c_bmw.wait()
    colw = iota((R, WIN), 1)
    bm_f = jnp.where((colw >= off) & (colw < off + BLK), bmw[...].astype(F32), 0.0)
    bmt[...] = tn(bm_f.astype(BF16), row_of_r).astype(BF16)
    for m in range(1, N_CHIP):
        k_x[m].wait_recv()
    grp_row = pl.multiple_of(core * (N_CHIP * TOK), N_CHIP * TOK)
    xc = xall[pl.ds(grp_row, N_CHIP * TOK), :]
    uc = nt(xc, at[...]).astype(BF16)
    urep[...] = nn(uc, row_of_r).astype(BF16)
    c_w1w.wait()
    for a in range(0, WIN, N_TILE):
        n = min(N_TILE, WIN - a)
        g[:, a : a + n] = gelu_slope(nn(xc, w1w[:, a : a + n]) + nn(uc, bmw[:, a : a + n]))
    k_g = rcopy(xall.at[pl.ds(grp_row, N_CHIP * TOK)], xall.at[pl.ds(grp_row, N_CHIP * TOK)], gs, gr, chip, mate)
    k_g.start()

    c_w2w.wait()
    lane_t = iota((TOK, R * T), 1) % T
    k_d = {}
    for step, m in enumerate(ORDER):
        buf = step % 2
        if m:
            k_e[m].wait_recv()
        slot = pl.multiple_of(peer(m) * TOK, TOK)
        e = eall[pl.ds(slot, TOK), :].astype(F32)
        for t in range(T):
            dz[buf, t * TOK : (t + 1) * TOK, :] = (
                e[:, t : t + 1] * hs[pl.ds(t, 1), :] + e[:, T + t : T + t + 1] * hs[pl.ds(T + t, 1), :]
            ).astype(BF16)
        for a in range(0, WIN, N_TILE):
            n = min(N_TILE, WIN - a)
            dh = nn(dz[buf], w2w[:, a : a + n]).reshape(T, TOK, n)
            dp[buf, :, a : a + n] = (dh * g[pl.ds(slot, TOK), a : a + n][None]).astype(BF16).reshape(T * TOK, n)
        du = nn(dp[buf], bmt[...])
        du = sum(jnp.where(lane_t == t, du[t * TOK : (t + 1) * TOK], 0.0) for t in range(T))
        if m:
            dsend[m] = du
            k_d[m] = rcopy(dsend.at[m], drecv.at[m], ds_.at[m], dr.at[m], peer(m), core)
            k_d[m].start()
        ur = urep[pl.ds(slot, TOK), :].astype(F32)
        ub = jnp.concatenate([jnp.where(lane_t == t, ur, 0.0).astype(BF16) for t in range(T)], axis=0)
        part = tn(ub, dp[buf])
        gb[...] = part if step == 0 else gb[...] + part

    ow0 = pl.multiple_of(core * (OWIN - 128), 128)
    mw0 = pl.multiple_of(mate * (OWIN - 128), 128)
    k_b = rcopy(gb.at[:, pl.ds(mw0, OWIN)], gbrecv, bs, br, chip, mate)
    k_b.start()
    for m in range(1, N_CHIP):
        k_d[m].wait_recv()
        du = du + drecv[m]
    duown[...] = du.astype(BF16)
    duall[pl.ds(my_row, TOK), :] = duown[...]
    others = [(m, o) for m in range(N_CHIP) for o in range(N_CORE) if m or o]
    k_n = []
    for i, (m, o) in enumerate(others):
        k_n.append(rcopy(duown, duall.at[pl.ds(my_row, TOK)], ns.at[i], nr.at[i], peer(m), mate if o else core))
        k_n[-1].start()

    k_b.wait_recv()
    off_own = off + 16 * core
    colo = iota((R * T, OWIN), 1)
    shard = (gb[:, pl.ds(ow0, OWIN)] + gbrecv[...]) * (1.0 / (N_CHIP * N_CORE * TOK))
    shard = jnp.where((colo >= off_own) & (colo < off_own + OWN), shard, 0.0)
    gbrecv[...] = shard
    lane = iota((T, 128), 1)
    sub = iota((T, 128), 0)
    parts = gram_parts([gbrecv[r * T : (r + 1) * T, :] for r in range(R)])
    row = sum(
        jnp.where(lane == T * k + sub, jnp.sum(p, axis=1, keepdims=True), 0.0) for k, p in enumerate(parts)
    )
    mown[...] = jnp.sum(row, axis=0, keepdims=True)
    mall[me] = mown[...]
    k_m = []
    for i, (m, o) in enumerate(others):
        k_m.append(rcopy(mown, mall.at[me], ms.at[i], mr.at[i], peer(m), mate if o else core))
        k_m[-1].start()

    k_g.wait_recv()
    for k in k_n:
        k.wait_recv()
    ga[:, :D] = tn(duall[...], xall[...]) * (1.0 / (N_CHIP * N_CORE * TOK))
    ga[:, D:] = jnp.zeros((R * T, DP - D), F32)
    parts = gram_parts([ga[r * T : (r + 1) * T, :] for r in range(R)])
    for k in k_m:
        k.wait_recv()
    mb = jnp.broadcast_to(sum(mall[i] for i in range(N_CHIP * N_CORE)), (T, 128))
    col = [
        jnp.sum(p + jnp.where(lane == T * k + sub, mb, 0.0), axis=1, keepdims=True) + jnp.zeros((T, 128), F32)
        for k, p in enumerate(parts)
    ]
    col += [pltpu.roll(col[T - k], k, 0) for k in range(5, T)]
    inv_scale = jnp.sum(col[0], axis=0, keepdims=True) / T

    def eg_step(_, w):
        grad = sum(col[k] * (w if k == 0 else pltpu.roll(w, k, 0)) for k in range(T))
        w = w * jnp.exp(-grad / inv_scale)
        return w / jnp.sum(w, axis=0, keepdims=True)

    w = lax.fori_loop(0, EG_STEPS, eg_step, jnp.full((T, 128), 1.0 / T, F32))
    alpha_out[...] = jnp.sum(jnp.where(lane == sub, w, 0.0), axis=0, keepdims=True)[:, :T]

    wcol = w[:, 0:1]
    dstart = (D // (N_CHIP * N_CORE)) * me
    dtile = dstart // 128
    da0 = pl.multiple_of(dtile * 128, 128)
    comb_a = jnp.concatenate(
        [jnp.sum(ga[r * T : (r + 1) * T, pl.ds(da0, 256)] * wcol, axis=0, keepdims=True) for r in range(R)], axis=0
    )
    ga_out[...] = pltpu.roll(comb_a, 256 - (dstart - da0), 1)[:, : D // (N_CHIP * N_CORE)]
    comb_b = jnp.concatenate(
        [jnp.sum(gbrecv[r * T : (r + 1) * T, :] * wcol, axis=0, keepdims=True) for r in range(R)], axis=0
    )
    gb_out[...] = pltpu.roll(comb_b, OWIN - off_own, 1)[:, :OWN]

    for k in [k_xp, k_g, k_b] + k_z + k_n + k_m + [k_x[m] for m in k_x] + [k_e[m] for m in k_e] + [k_d[m] for m in k_d]:
        k.wait_send()


def solution(mesh):
    n_dev = mesh.shape["data"]
    assert n_dev == N_CHIP * N_CORE
    vm = pltpu.VMEM
    dma = pltpu.SemaphoreType.DMA
    scratch = [
        vm((D, HALF), BF16), vm((DP, HALF), BF16), vm((D, WIN), BF16), vm((D, WIN), BF16),
        vm((R, HALF), BF16), vm((R, WIN), BF16), vm((R, D), BF16), vm((T, C, D), BF16), vm((T, TOK), jnp.int32),
        vm((2 * TOK, D), BF16), vm((n_dev * TOK, D), BF16), vm((128, HALF), BF16),
        vm((C * T, D), F32), vm((C * T, D), BF16), vm((C * T, D), BF16),
        vm((WIN, R * T), BF16), vm((N_CHIP * TOK, R * T), BF16), vm((N_CHIP * TOK, WIN), F32),
        vm((TOK, DP), F32), vm((TOK, DP), F32), vm((TOK, DP), F32),
        vm((TOK, 128), BF16), vm((N_CHIP * TOK, 128), BF16),
        vm((2, T * TOK, D), BF16), vm((2, T * TOK, WIN), BF16),
        vm((N_CHIP, TOK, R * T), F32), vm((N_CHIP, TOK, R * T), F32),
        vm((TOK, R * T), BF16), vm((n_dev * TOK, R * T), BF16),
        vm((R * T, WIN), F32), vm((R * T, OWIN), F32),
        vm((1, 128), F32), vm((n_dev, 1, 128), F32), vm((R * T, DP), F32),
        dma((16,)), dma((N_CHIP,)), dma((N_CHIP,)), dma, dma, dma((4,)), dma((4,)),
        dma((N_CHIP,)), dma((N_CHIP,)), dma((N_CHIP,)), dma((N_CHIP,)), dma, dma,
        dma((n_dev,)), dma((n_dev,)), dma((n_dev,)), dma((n_dev,)), dma, dma,
    ]

    def device_step(tokens, labels, w_one, w_two, adapter_a, adapter_b, task_heads):
        call = pl.pallas_call(
            kernel,
            out_shape=(
                jax.ShapeDtypeStruct((1, T), F32),
                jax.ShapeDtypeStruct((R, D // n_dev), F32),
                jax.ShapeDtypeStruct((R, FF // n_dev), F32),
            ),
            in_specs=[pl.BlockSpec(memory_space=pltpu.HBM)] * 7,
            out_specs=tuple([pl.BlockSpec(memory_space=pltpu.VMEM)] * 3),
            scratch_shapes=scratch,
            compiler_params=pltpu.CompilerParams(
                collective_id=0, has_side_effects=True, vmem_limit_bytes=60 * 1024 * 1024
            ),
            name="min_norm",
        )
        alpha, ga_t, gb = call(
            tokens, labels, w_one, w_two.T, adapter_a.T, adapter_b, task_heads.transpose(0, 2, 1)
        )
        return alpha.reshape(T), ga_t.T, gb

    return jax.shard_map(
        device_step,
        mesh=mesh,
        in_specs=(P("data", None), P(None, "data"), P(), P(), P(), P(), P()),
        out_specs=(P(), P("data", None), P(None, "data")),
        check_vma=False,
    )
```

time: 253 us -> 46.6 us (0.18)
  waiting for transfers between devices: 98.7 us -> 0 us
  matrix products: 43.4 us -> 0 us
  Pallas kernels: 0 us -> 41.9 us
  other arithmetic: 31.7 us -> 0 us
  blocking collectives: 30.9 us -> 0 us
  local copies, waits for them, and re-layouts: 31.3 us -> 3.81 us
  between operations: 14.9 us -> 0.64 us
    unnamed x4 -> x0, waiting for transfers between devices: 98.7 us -> none
    dot_general x9 -> x0, matrix products: 43.4 us -> none  [the longest x1 13 us: task_grads(): jnp.einsum('bd,tdc->tbc', trunk_out, task_heads, preferred_element_type=j...]
    pallas_call x0 -> x1, Pallas kernels: none -> 41.9 us  [device_step(): call(tokens, labels, w_one, w_two.T, adapter_a.T, adapter_b, task_heads.t...]
    psum x1 -> x0, blocking collectives: 30.9 us -> none  [device_step(): gram_mat = lax.psum(gram_part, 'data')]
    unnamed x18 -> x3, local copies, waits for them, and re-layouts: 31.3 us -> 3.81 us
    reduce_sum x44 -> x0, other arithmetic: 17.6 us -> none  [the longest x20 12.4 us: eg_step(): return weights / jnp.sum(weights)]
    div x22 -> x0, other arithmetic: 14 us -> none  [the longest x20 13 us: eg_step(): return weights / jnp.sum(weights)]
  transfers between devices with their start and end apart: 2 -> 0, of which waited for: 2 -> 0; matrix products, arithmetic and copies ran while one was open for 13% -> 0% of each run, Pallas kernels for 0% -> 0%
where the time goes in v1:
time: 46.6 us; the launch traced here: 46.4 us
  Pallas kernels  41.9 us (90%)
  local copies, waits for them, and re-layouts  3.81 us (8%)
  between operations  0.64 us (1%)
    pallas_call x1, Pallas kernels, device_step(): call(tokens, labels, w_one, w_two.T, adapter_a.T, adapter_b, task_heads.t...  41.9 us
    unnamed x3, local copies, waits for them, and re-layouts  3.81 us

profile of v1, /device:TPU:0, one launch (start us, length us, event | category | flops | bytes accessed | tf_op | source)
XLA Modules:
  0.0 46.4 jit_solution(15004553586413562030)
XLA Ops:
  0.6 41.9 %min_norm.1 = (f32[1,8]{1,0:T(1,128)}, f32[16,100]{1,0:T(8,128)}, f32[16,400]{1,0:T(8,128)}) custom-call(bf16[32,1600]{1,0:T(8,128)(2,1)} %x_hbm.1, s32[8,32]{1,0:T(8,128)} %lab_hbm.1, bf16[1600,6400]{1,0:T(8,128)(2,1)} %w1_hbm.1, bf16[1600,6400]{1,0:T(8,128)(2,1)} %bitcast.5, bf16[16,1600]{1,0:T(8,128)(2,1)} %bitcast.6, bf16[16,6400]{1,0:T(8,128)(2,1)} %bm_hbm.1, ...), custom_call_target="tpu_custom_call" | custom-call | tf_op jit(solution)/shard_map/min_norm/pallas_call | solution.py:345
  42.6 1.1 %copy.13 = f32[8]{0:T(128)} copy(f32[8]{0:T(128)} %bitcast.9) | data formatting | bytes 64
  43.7 1.3 %copy.14 = f32[100,16]{0,1:T(8,128)} copy(f32[100,16]{0,1:T(8,128)} %bitcast.8) | data formatting | bytes 12800
  45.0 1.4 %copy.15 = f32[16,400]{1,0:T(8,128)} copy(f32[16,400]{1,0:T(8,128)} %get-tuple-element.14) | data formatting | bytes 51200

commit v2 on v1

--- a/solution.py
+++ b/solution.py
@@ -20,8 +20,9 @@
 WIN = 896
 OWIN = 512
 W1_CHUNKS = ((0, 768), (768, 768), (1536, 768), (2304, 896))
-W2_CHUNKS = ((0, 512), (512, 512), (1024, 512), (1536, 128))
-ORDER = (1, 3, 5, 7, 6, 2, 4, 0)
+W2_CHUNKS = ((0, 512), (512, 512), (1024, 256), (1280, 320))
+NEAR, FAR = (0, 1, 2, 4), (3, 5, 6, 7)
+BLOCKS = ((0,), (1, 2), (3, 5, 6, 7), (4,))
 GELU_C = 0.7978845608028654
 N_TILE = 256
 
@@ -67,7 +68,7 @@
     x_hbm, lab_hbm, w1_hbm, w2_hbm, at_hbm, bm_hbm, hd_hbm,
     alpha_out, ga_out, gb_out,
     w1h, w2h, w1w, w2w, bmh, bmw, at, hd, lab, xp, xall, hbuf, hs, ha, hb, bmt, urep, g,
-    zown, zsend, zrecv, eown, eall, dz, dp, dsend, drecv, duown, duall, gb, gbrecv, mown, mall, ga,
+    zown, zsend, zrecv, eown, eall, dz, dp, ub, dsend, drecv, duown, duall, gb, gbrecv, mown, mall, ga,
     lsem, xs, xr, ps, pr, zs, zr, es, er, ds_, dr, bs, br, ns, nr, ms, mr, gs, gr,
 ):
     me = lax.axis_index("data")
@@ -105,11 +106,10 @@
     c_lab = load(lab_hbm, lab)
     c_bmh = load(bm_hbm.at[:, pl.ds(half0, HALF)], bmh)
     c_w1 = [load(w1_hbm.at[:, pl.ds(pl.multiple_of(half0 + a, 128), n)], w1h.at[:, pl.ds(a, n)]) for a, n in W1_CHUNKS]
-    c_w2 = [
-        load(w2_hbm.at[pl.ds(a, min(n, D - a)), pl.ds(half0, HALF)], w2h.at[pl.ds(a, min(n, D - a))]) for a, n in W2_CHUNKS
-    ]
+    c_w2 = [load(w2_hbm.at[pl.ds(a, n), pl.ds(half0, HALF)], w2h.at[pl.ds(a, n)]) for a, n in W2_CHUNKS[:-1]]
     c_bmw = load(bm_hbm.at[:, pl.ds(win0, WIN)], bmw)
     c_w1w = load(w1_hbm.at[:, pl.ds(win0, WIN)], w1w)
+    c_w2 += [load(w2_hbm.at[pl.ds(a, n), pl.ds(half0, HALF)], w2h.at[pl.ds(a, n)]) for a, n in W2_CHUNKS[-1:]]
     c_w2w = load(w2_hbm.at[:, pl.ds(win0, WIN)], w2w)
 
     barrier = pltpu.get_barrier_semaphore()
@@ -120,8 +120,6 @@
                     barrier, inc=1, device_id=(N_CORE * peer(m) + (mate if other else core),), device_id_type=MESH
                 )
 
-    hbuf[...] = jnp.zeros_like(hbuf)
-    w2h[pl.ds(D, DP - D), :] = jnp.zeros((DP - D, HALF), BF16)
     eown[...] = jnp.zeros_like(eown)
     row_of_r = (iota((R, R * T), 1) // T == iota((R, R * T), 0)).astype(F32).astype(BF16)
     c_hd.wait()
@@ -156,21 +154,49 @@
     c_bmh.wait()
     for (a, n), cp in zip(W1_CHUNKS, c_w1):
         cp.wait()
-        pre = nn(x2, w1h[:, a : a + n]) + nn(u2, bmh[:, a : a + n])
-        hbuf[pl.ds(0, 2 * TOK), a : a + n] = gelu(pre).astype(BF16)
+        for i in range(a, a + n, N_TILE):
+            j = min(i + N_TILE, a + n)
+            pre = nn(x2, w1h[:, i:j]) + nn(u2, bmh[:, i:j])
+            hbuf[:, i:j] = gelu(pre).astype(BF16)
     k_z = []
+    cut = HALF // 256 * 128
     for i, ((a, n), cp) in enumerate(zip(W2_CHUNKS, c_w2)):
         cp.wait()
-        zt = nt(w2h[pl.ds(a, n), :], hbuf[...])
-        z = jnp.transpose(zt)
+        if n == 2 * N_TILE:
+            z = nt(hbuf[...], w2h[pl.ds(a, n), :])
+        else:
+            z = nt(hbuf[:, :cut], w2h[pl.ds(a, n), :cut]) + nt(hbuf[:, cut:], w2h[pl.ds(a, n), cut:])
         zown[:, a : a + n] = z[:TOK]
-        zsend[:, a : a + n] = z[TOK : 2 * TOK]
+        zsend[:, a : a + n] = z[TOK:]
         k_z.append(rcopy(zsend.at[:, pl.ds(a, n)], zrecv.at[:, pl.ds(a, n)], zs.at[i], zr.at[i], chip, mate))
         k_z[-1].start()
+
+    c_bmw.wait()
+    colw = iota((R, WIN), 1)
+    bm_f = jnp.where((colw >= off) & (colw < off + BLK), bmw[...].astype(F32), 0.0)
+    bmt[...] = tn(bm_f.astype(BF16), row_of_r).astype(BF16)
+    grp_row = pl.multiple_of(core * (N_CHIP * TOK), N_CHIP * TOK)
+    c_w1w.wait()
+
+    def slopes(which, base):
+        for m in which:
+            if m:
+                k_x[m].wait_recv()
+        xc = jnp.concatenate(
+            [xall[pl.ds(pl.multiple_of(grp_row + peer(m) * TOK, TOK), TOK), :] for m in which], axis=0
+        )
+        n_row = len(which) * TOK
+        uc = nt(xc, at[...]).astype(BF16)
+        urep[base : base + n_row, :] = nn(uc, row_of_r).astype(BF16)
+        for a in range(0, WIN, N_TILE):
+            n = min(N_TILE, WIN - a)
+            g[base : base + n_row, a : a + n] = gelu_slope(nn(xc, w1w[:, a : a + n]) + nn(uc, bmw[:, a : a + n]))
+
+    slopes(NEAR, 0)
     for k in k_z:
         k.wait_recv()
     xf = xp[pl.ds(0, TOK), :].astype(F32)
-    zb = (xf + (zown[:, :D] + zrecv[:, :D])).astype(BF16)
+    zb = (xf + (zown[...] + zrecv[...])).astype(BF16)
     la, lb = nt(zb, ha[...]), nt(zb, hb[...])
     top = jnp.maximum(la, lb)
     ea, eb = jnp.exp(la - top), jnp.exp(lb - top)
@@ -183,50 +209,52 @@
         k_e[m] = rcopy(eown, eall.at[pl.ds(my_slot, TOK)], es.at[m], er.at[m], peer(m), core)
         k_e[m].start()
 
-    c_bmw.wait()
-    colw = iota((R, WIN), 1)
-    bm_f = jnp.where((colw >= off) & (colw < off + BLK), bmw[...].astype(F32), 0.0)
-    bmt[...] = tn(bm_f.astype(BF16), row_of_r).astype(BF16)
-    for m in range(1, N_CHIP):
-        k_x[m].wait_recv()
-    grp_row = pl.multiple_of(core * (N_CHIP * TOK), N_CHIP * TOK)
-    xc = xall[pl.ds(grp_row, N_CHIP * TOK), :]
-    uc = nt(xc, at[...]).astype(BF16)
-    urep[...] = nn(uc, row_of_r).astype(BF16)
-    c_w1w.wait()
-    for a in range(0, WIN, N_TILE):
-        n = min(N_TILE, WIN - a)
-        g[:, a : a + n] = gelu_slope(nn(xc, w1w[:, a : a + n]) + nn(uc, bmw[:, a : a + n]))
+    c_w2w.wait()
+    lane_t = iota((TOK, R * T), 1) % T
+    rel = {m: i * TOK for i, m in enumerate(NEAR + FAR)}
+    k_d = {}
+
+    def backward(block, first):
+        for i, m in enumerate(block):
+            if m:
+                k_e[m].wait_recv()
+        dus = {}
+        for i, m in enumerate(block):
+            r0 = i * T * TOK
+            e = eall[pl.ds(pl.multiple_of(peer(m) * TOK, TOK), TOK), :].astype(F32)
+            for t in range(T):
+                dz[i, t * TOK : (t + 1) * TOK, :] = (
+                    e[:, t : t + 1] * hs[pl.ds(t, 1), :] + e[:, T + t : T + t + 1] * hs[pl.ds(T + t, 1), :]
+                ).astype(BF16)
+            for a in range(0, WIN, N_TILE):
+                n = min(N_TILE, WIN - a)
+                dh = nn(dz[i], w2w[:, a : a + n]).reshape(T, TOK, n)
+                slope = g[rel[m] : rel[m] + TOK, a : a + n]
+                dp[r0 : r0 + T * TOK, a : a + n] = (dh * slope[None]).astype(BF16).reshape(T * TOK, n)
+            du = nn(dp[r0 : r0 + T * TOK, :], bmt[...])
+            dus[m] = sum(jnp.where(lane_t == t, du[t * TOK : (t + 1) * TOK], 0.0) for t in range(T))
+            if m:
+                dsend[m] = dus[m]
+            ur = urep[rel[m] : rel[m] + TOK, :].astype(F32)
+            for t in range(T):
+                ub[r0 + t * TOK : r0 + (t + 1) * TOK, :] = jnp.where(lane_t == t, ur, 0.0).astype(BF16)
+        n_row = len(block) * T * TOK
+        for a in range(0, WIN, N_TILE):
+            n = min(N_TILE, WIN - a)
+            part = tn(ub[:n_row, :], dp[:n_row, a : a + n])
+            gb[:, a : a + n] = part if first else gb[:, a : a + n] + part
+        for m in block:
+            if m:
+                k_d[m] = rcopy(dsend.at[m], drecv.at[m], ds_.at[m], dr.at[m], peer(m), core)
+                k_d[m].start()
+        return dus
+
+    du_own = backward(BLOCKS[0], True)[0]
+    slopes(FAR, len(NEAR) * TOK)
     k_g = rcopy(xall.at[pl.ds(grp_row, N_CHIP * TOK)], xall.at[pl.ds(grp_row, N_CHIP * TOK)], gs, gr, chip, mate)
     k_g.start()
-
-    c_w2w.wait()
-    lane_t = iota((TOK, R * T), 1) % T
-    k_d = {}
-    for step, m in enumerate(ORDER):
-        buf = step % 2
-        if m:
-            k_e[m].wait_recv()
-        slot = pl.multiple_of(peer(m) * TOK, TOK)
-        e = eall[pl.ds(slot, TOK), :].astype(F32)
-        for t in range(T):
-            dz[buf, t * TOK : (t + 1) * TOK, :] = (
-                e[:, t : t + 1] * hs[pl.ds(t, 1), :] + e[:, T + t : T + t + 1] * hs[pl.ds(T + t, 1), :]
-            ).astype(BF16)
-        for a in range(0, WIN, N_TILE):
-            n = min(N_TILE, WIN - a)
-            dh = nn(dz[buf], w2w[:, a : a + n]).reshape(T, TOK, n)
-            dp[buf, :, a : a + n] = (dh * g[pl.ds(slot, TOK), a : a + n][None]).astype(BF16).reshape(T * TOK, n)
-        du = nn(dp[buf], bmt[...])
-        du = sum(jnp.where(lane_t == t, du[t * TOK : (t + 1) * TOK], 0.0) for t in range(T))
-        if m:
-            dsend[m] = du
-            k_d[m] = rcopy(dsend.at[m], drecv.at[m], ds_.at[m], dr.at[m], peer(m), core)
-            k_d[m].start()
-        ur = urep[pl.ds(slot, TOK), :].astype(F32)
-        ub = jnp.concatenate([jnp.where(lane_t == t, ur, 0.0).astype(BF16) for t in range(T)], axis=0)
-        part = tn(ub, dp[buf])
-        gb[...] = part if step == 0 else gb[...] + part
+    for block in BLOCKS[1:]:
+        backward(block, False)
 
     ow0 = pl.multiple_of(core * (OWIN - 128), 128)
     mw0 = pl.multiple_of(mate * (OWIN - 128), 128)
@@ -234,8 +262,8 @@
     k_b.start()
     for m in range(1, N_CHIP):
         k_d[m].wait_recv()
-        du = du + drecv[m]
-    duown[...] = du.astype(BF16)
+        du_own = du_own + drecv[m]
+    duown[...] = du_own.astype(BF16)
     duall[pl.ds(my_row, TOK), :] = duown[...]
     others = [(m, o) for m in range(N_CHIP) for o in range(N_CORE) if m or o]
     k_n = []
@@ -275,12 +303,13 @@
         jnp.sum(p + jnp.where(lane == T * k + sub, mb, 0.0), axis=1, keepdims=True) + jnp.zeros((T, 128), F32)
         for k, p in enumerate(parts)
     ]
+    scale = jnp.sum(col[0], axis=0, keepdims=True) / T
+    col = [c / scale for c in col]
     col += [pltpu.roll(col[T - k], k, 0) for k in range(5, T)]
-    inv_scale = jnp.sum(col[0], axis=0, keepdims=True) / T
 
     def eg_step(_, w):
         grad = sum(col[k] * (w if k == 0 else pltpu.roll(w, k, 0)) for k in range(T))
-        w = w * jnp.exp(-grad / inv_scale)
+        w = w * jnp.exp(-grad)
         return w / jnp.sum(w, axis=0, keepdims=True)
 
     w = lax.fori_loop(0, EG_STEPS, eg_step, jnp.full((T, 128), 1.0 / T, F32))
@@ -303,20 +332,29 @@
         k.wait_send()
 
 
+def put_kernel(alpha_in, ga_in, gb_in, alpha_out, ga_out, gb_out, sem):
+    pairs = ((alpha_in, alpha_out), (ga_in, ga_out), (gb_in, gb_out))
+    copies = [pltpu.make_async_copy(a, b, sem.at[i]) for i, (a, b) in enumerate(pairs)]
+    for c in copies:
+        c.start()
+    for c in copies:
+        c.wait()
+
+
 def solution(mesh):
     n_dev = mesh.shape["data"]
     assert n_dev == N_CHIP * N_CORE
     vm = pltpu.VMEM
     dma = pltpu.SemaphoreType.DMA
     scratch = [
-        vm((D, HALF), BF16), vm((DP, HALF), BF16), vm((D, WIN), BF16), vm((D, WIN), BF16),
+        vm((D, HALF), BF16), vm((D, HALF), BF16), vm((D, WIN), BF16), vm((D, WIN), BF16),
         vm((R, HALF), BF16), vm((R, WIN), BF16), vm((R, D), BF16), vm((T, C, D), BF16), vm((T, TOK), jnp.int32),
-        vm((2 * TOK, D), BF16), vm((n_dev * TOK, D), BF16), vm((128, HALF), BF16),
+        vm((2 * TOK, D), BF16), vm((n_dev * TOK, D), BF16), vm((2 * TOK, HALF), BF16),
         vm((C * T, D), F32), vm((C * T, D), BF16), vm((C * T, D), BF16),
         vm((WIN, R * T), BF16), vm((N_CHIP * TOK, R * T), BF16), vm((N_CHIP * TOK, WIN), F32),
-        vm((TOK, DP), F32), vm((TOK, DP), F32), vm((TOK, DP), F32),
+        vm((TOK, D), F32), vm((TOK, D), F32), vm((TOK, D), F32),
         vm((TOK, 128), BF16), vm((N_CHIP * TOK, 128), BF16),
-        vm((2, T * TOK, D), BF16), vm((2, T * TOK, WIN), BF16),
+        vm((4, T * TOK, D), BF16), vm((4 * T * TOK, WIN), BF16), vm((4 * T * TOK, R * T), BF16),
         vm((N_CHIP, TOK, R * T), F32), vm((N_CHIP, TOK, R * T), F32),
         vm((TOK, R * T), BF16), vm((n_dev * TOK, R * T), BF16),
         vm((R * T, WIN), F32), vm((R * T, OWIN), F32),
@@ -327,13 +365,10 @@
     ]
 
     def device_step(tokens, labels, w_one, w_two, adapter_a, adapter_b, task_heads):
+        out_shapes = ((1, T), (R, D // n_dev), (R, FF // n_dev))
         call = pl.pallas_call(
             kernel,
-            out_shape=(
-                jax.ShapeDtypeStruct((1, T), F32),
-                jax.ShapeDtypeStruct((R, D // n_dev), F32),
-                jax.ShapeDtypeStruct((R, FF // n_dev), F32),
-            ),
+            out_shape=tuple(pltpu.VMEM(s, F32) for s in out_shapes),
             in_specs=[pl.BlockSpec(memory_space=pltpu.HBM)] * 7,
             out_specs=tuple([pl.BlockSpec(memory_space=pltpu.VMEM)] * 3),
             scratch_shapes=scratch,
@@ -342,9 +377,19 @@
             ),
             name="min_norm",
         )
-        alpha, ga_t, gb = call(
+        put = pl.pallas_call(
+            put_kernel,
+            out_shape=tuple(jax.ShapeDtypeStruct(s, F32) for s in out_shapes),
+            in_specs=[pl.BlockSpec(memory_space=pltpu.VMEM)] * 3,
+            out_specs=tuple([pl.BlockSpec(memory_space=pltpu.HBM)] * 3),
+            scratch_shapes=[dma((3,))],
+            compiler_params=pltpu.CompilerParams(vmem_limit_bytes=1024 * 1024),
+            name="put",
+        )
+        results = call(
             tokens, labels, w_one, w_two.T, adapter_a.T, adapter_b, task_heads.transpose(0, 2, 1)
         )
+        alpha, ga_t, gb = put(*results)
         return alpha.reshape(T), ga_t.T, gb
 
     return jax.shard_map(

time: 46.6 us -> 39.6 us (0.85)
  local copies, waits for them, and re-layouts: 3.81 us -> 0 us
  Pallas kernels: 41.9 us -> 38.7 us
    pallas_call x1, Pallas kernels: 41.9 us -> 38.1 us  [device_step(): call(tokens, labels, w_one, w_two.T, adapter_a.T, adapter_b, task_heads.t...]
    unnamed x3 -> x0, local copies, waits for them, and re-layouts: 3.81 us -> none
    pallas_call x0 -> x1, Pallas kernels: none -> 0.65 us  [device_step(): alpha, ga_t, gb = put(*results)]
where the time goes in v2:
time: 39.6 us; the launch traced here: 39.5 us
  Pallas kernels  38.7 us (98%)
  between operations  0.8 us (2%)
    pallas_call x1, Pallas kernels, device_step(): call(tokens, labels, w_one, w_two.T, adapter_a.T, adapter_b, task_heads.t...  38.1 us

profile of v2, /device:TPU:0, one launch (start us, length us, event | category | flops | bytes accessed | tf_op | source)
XLA Modules:
  0.0 39.5 jit_solution(12623397025140120781)
XLA Ops:
  0.6 38.1 %min_norm.1 = (f32[1,8]{1,0:T(1,128)S(1)}, f32[16,100]{1,0:T(8,128)S(1)}, f32[16,400]{1,0:T(8,128)S(1)}) custom-call(bf16[32,1600]{1,0:T(8,128)(2,1)} %x_hbm.1, s32[8,32]{1,0:T(8,128)} %lab_hbm.1, bf16[1600,6400]{1,0:T(8,128)(2,1)} %w1_hbm.1, bf16[1600,6400]{1,0:T(8,128)(2,1)} %bitcast.5, bf16[16,1600]{1,0:T(8,128)(2,1)} %bitcast.6, ...), custom_call_target="tpu_custom_call" | custom-call | tf_op jit(solution)/shard_map/min_norm/pallas_call | solution.py:389
  38.7 0.7 %put.1 = (f32[1,8]{1,0:T(1,128)}, f32[16,100]{1,0:T(8,128)}, f32[16,400]{1,0:T(8,128)}) custom-call(f32[1,8]{1,0:T(1,128)S(1)} %get-tuple-element.9.alpha_in, f32[16,100]{1,0:T(8,128)S(1)} %get-tuple-element.10.ga_in, f32[16,400]{1,0:T(8,128)S(1)} %get-tuple-element.11.gb_in), custom_call_target="tpu_custom_call" | custom-call | tf_op jit(solution)/shard_map/put/pallas_call | solution.py:392

commit v3 on v2

--- a/solution.py
+++ b/solution.py
@@ -19,8 +19,8 @@
 OWN = BLK // N_CORE
 WIN = 896
 OWIN = 512
-W1_CHUNKS = ((0, 768), (768, 768), (1536, 768), (2304, 896))
-W2_CHUNKS = ((0, 512), (512, 512), (1024, 256), (1280, 320))
+W1_CHUNKS = ((0, 1536), (1536, 1664))
+W2_CHUNKS = ((0, 1024), (1024, 576))
 NEAR, FAR = (0, 1, 2, 4), (3, 5, 6, 7)
 BLOCKS = ((0,), (1, 2), (3, 5, 6, 7), (4,))
 GELU_C = 0.7978845608028654
@@ -67,7 +67,7 @@
 def kernel(
     x_hbm, lab_hbm, w1_hbm, w2_hbm, at_hbm, bm_hbm, hd_hbm,
     alpha_out, ga_out, gb_out,
-    w1h, w2h, w1w, w2w, bmh, bmw, at, hd, lab, xp, xall, hbuf, hs, ha, hb, bmt, urep, g,
+    w1h, w2h, w1w, w2w, bmh, bmw, at, hd, lab, xp, xall, hbuf, hs, ha, hb, bmt, bms, urep, g,
     zown, zsend, zrecv, eown, eall, dz, dp, ub, dsend, drecv, duown, duall, gb, gbrecv, mown, mall, ga,
     lsem, xs, xr, ps, pr, zs, zr, es, er, ds_, dr, bs, br, ns, nr, ms, mr, gs, gr,
 ):
@@ -105,11 +105,10 @@
     c_hd = load(hd_hbm, hd)
     c_lab = load(lab_hbm, lab)
     c_bmh = load(bm_hbm.at[:, pl.ds(half0, HALF)], bmh)
+    c_bmw = load(bm_hbm.at[:, pl.ds(win0, WIN)], bmw)
     c_w1 = [load(w1_hbm.at[:, pl.ds(pl.multiple_of(half0 + a, 128), n)], w1h.at[:, pl.ds(a, n)]) for a, n in W1_CHUNKS]
-    c_w2 = [load(w2_hbm.at[pl.ds(a, n), pl.ds(half0, HALF)], w2h.at[pl.ds(a, n)]) for a, n in W2_CHUNKS[:-1]]
-    c_bmw = load(bm_hbm.at[:, pl.ds(win0, WIN)], bmw)
-    c_w1w = load(w1_hbm.at[:, pl.ds(win0, WIN)], w1w)
-    c_w2 += [load(w2_hbm.at[pl.ds(a, n), pl.ds(half0, HALF)], w2h.at[pl.ds(a, n)]) for a, n in W2_CHUNKS[-1:]]
+    c_w2 = [load(w2_hbm.at[pl.ds(a, n), pl.ds(half0, HALF)], w2h.at[pl.ds(a, n)]) for a, n in W2_CHUNKS]
+    c_w1w = load(w1_hbm.at[:, pl.ds(win0, WIN)], w1w.at[:, pl.ds(0, WIN)])
     c_w2w = load(w2_hbm.at[:, pl.ds(win0, WIN)], w2w)
 
     barrier = pltpu.get_barrier_semaphore()
@@ -148,6 +147,14 @@
         k_x[m].start()
 
     c_at.wait()
+    w1w[:, WIN:] = tn(at[...], row_of_r).astype(BF16)
+    c_bmw.wait()
+    colw = iota((R, WIN), 1)
+    bm_f = jnp.where((colw >= off) & (colw < off + BLK), bmw[...].astype(F32), 0.0)
+    bmt[...] = tn(bm_f.astype(BF16), row_of_r).astype(BF16)
+    first_of_r = (T * iota((R, R * T), 0) == iota((R, R * T), 1)).astype(F32).astype(BF16)
+    bms[...] = tn(first_of_r, bmw[...]).astype(BF16)
+
     k_xp.wait_recv()
     x2 = xp[...]
     u2 = nt(x2, at[...]).astype(BF16)
@@ -159,22 +166,15 @@
             pre = nn(x2, w1h[:, i:j]) + nn(u2, bmh[:, i:j])
             hbuf[:, i:j] = gelu(pre).astype(BF16)
     k_z = []
-    cut = HALF // 256 * 128
     for i, ((a, n), cp) in enumerate(zip(W2_CHUNKS, c_w2)):
         cp.wait()
-        if n == 2 * N_TILE:
-            z = nt(hbuf[...], w2h[pl.ds(a, n), :])
-        else:
-            z = nt(hbuf[:, :cut], w2h[pl.ds(a, n), :cut]) + nt(hbuf[:, cut:], w2h[pl.ds(a, n), cut:])
-        zown[:, a : a + n] = z[:TOK]
-        zsend[:, a : a + n] = z[TOK:]
+        for j in range(a, a + n, N_TILE):
+            z = nt(hbuf[...], w2h[j : min(j + N_TILE, a + n), :])
+            zown[:, j : min(j + N_TILE, a + n)] = z[:TOK]
+            zsend[:, j : min(j + N_TILE, a + n)] = z[TOK:]
         k_z.append(rcopy(zsend.at[:, pl.ds(a, n)], zrecv.at[:, pl.ds(a, n)], zs.at[i], zr.at[i], chip, mate))
         k_z[-1].start()
 
-    c_bmw.wait()
-    colw = iota((R, WIN), 1)
-    bm_f = jnp.where((colw >= off) & (colw < off + BLK), bmw[...].astype(F32), 0.0)
-    bmt[...] = tn(bm_f.astype(BF16), row_of_r).astype(BF16)
     grp_row = pl.multiple_of(core * (N_CHIP * TOK), N_CHIP * TOK)
     c_w1w.wait()
 
@@ -186,11 +186,15 @@
             [xall[pl.ds(pl.multiple_of(grp_row + peer(m) * TOK, TOK), TOK), :] for m in which], axis=0
         )
         n_row = len(which) * TOK
-        uc = nt(xc, at[...]).astype(BF16)
-        urep[base : base + n_row, :] = nn(uc, row_of_r).astype(BF16)
-        for a in range(0, WIN, N_TILE):
-            n = min(N_TILE, WIN - a)
-            g[base : base + n_row, a : a + n] = gelu_slope(nn(xc, w1w[:, a : a + n]) + nn(uc, bmw[:, a : a + n]))
+        last = WIN - WIN % N_TILE
+        pre = nn(xc, w1w[:, last:])
+        ur = pre[:, WIN - last :].astype(BF16)
+        urep[base : base + n_row, :] = ur
+        pre = pre[:, : WIN - last] + nn(ur, bms[:, last:])
+        g[base : base + n_row, last:] = gelu_slope(pre)
+        for a in range(0, last, N_TILE):
+            pre = nn(xc, w1w[:, a : a + N_TILE]) + nn(ur, bms[:, a : a + N_TILE])
+            g[base : base + n_row, a : a + N_TILE] = gelu_slope(pre)
 
     slopes(NEAR, 0)
     for k in k_z:
@@ -214,21 +218,21 @@
     rel = {m: i * TOK for i, m in enumerate(NEAR + FAR)}
     k_d = {}
 
-    def backward(block, first):
-        for i, m in enumerate(block):
+    def backward(block):
+        for m in block:
             if m:
                 k_e[m].wait_recv()
         dus = {}
-        for i, m in enumerate(block):
-            r0 = i * T * TOK
+        for m in block:
+            r0 = rel[m] * T
             e = eall[pl.ds(pl.multiple_of(peer(m) * TOK, TOK), TOK), :].astype(F32)
             for t in range(T):
-                dz[i, t * TOK : (t + 1) * TOK, :] = (
+                dz[rel[m] // TOK % 4, t * TOK : (t + 1) * TOK, :] = (
                     e[:, t : t + 1] * hs[pl.ds(t, 1), :] + e[:, T + t : T + t + 1] * hs[pl.ds(T + t, 1), :]
                 ).astype(BF16)
             for a in range(0, WIN, N_TILE):
                 n = min(N_TILE, WIN - a)
-                dh = nn(dz[i], w2w[:, a : a + n]).reshape(T, TOK, n)
+                dh = nn(dz[rel[m] // TOK % 4], w2w[:, a : a + n]).reshape(T, TOK, n)
                 slope = g[rel[m] : rel[m] + TOK, a : a + n]
                 dp[r0 : r0 + T * TOK, a : a + n] = (dh * slope[None]).astype(BF16).reshape(T * TOK, n)
             du = nn(dp[r0 : r0 + T * TOK, :], bmt[...])
@@ -238,23 +242,21 @@
             ur = urep[rel[m] : rel[m] + TOK, :].astype(F32)
             for t in range(T):
                 ub[r0 + t * TOK : r0 + (t + 1) * TOK, :] = jnp.where(lane_t == t, ur, 0.0).astype(BF16)
-        n_row = len(block) * T * TOK
-        for a in range(0, WIN, N_TILE):
-            n = min(N_TILE, WIN - a)
-            part = tn(ub[:n_row, :], dp[:n_row, a : a + n])
-            gb[:, a : a + n] = part if first else gb[:, a : a + n] + part
         for m in block:
             if m:
                 k_d[m] = rcopy(dsend.at[m], drecv.at[m], ds_.at[m], dr.at[m], peer(m), core)
                 k_d[m].start()
         return dus
 
-    du_own = backward(BLOCKS[0], True)[0]
-    slopes(FAR, len(NEAR) * TOK)
-    k_g = rcopy(xall.at[pl.ds(grp_row, N_CHIP * TOK)], xall.at[pl.ds(grp_row, N_CHIP * TOK)], gs, gr, chip, mate)
-    k_g.start()
+    du_own = backward(BLOCKS[0])[0]
     for block in BLOCKS[1:]:
-        backward(block, False)
+        if block == FAR:
+            slopes(FAR, len(NEAR) * TOK)
+            k_g = rcopy(xall.at[pl.ds(grp_row, N_CHIP * TOK)], xall.at[pl.ds(grp_row, N_CHIP * TOK)], gs, gr, chip, mate)
+            k_g.start()
+        backward(block)
+    for a in range(0, WIN, N_TILE):
+        gb[:, a : min(a + N_TILE, WIN)] = tn(ub[...], dp[:, a : min(a + N_TILE, WIN)])
 
     ow0 = pl.multiple_of(core * (OWIN - 128), 128)
     mw0 = pl.multiple_of(mate * (OWIN - 128), 128)
@@ -265,7 +267,7 @@
         du_own = du_own + drecv[m]
     duown[...] = du_own.astype(BF16)
     duall[pl.ds(my_row, TOK), :] = duown[...]
-    others = [(m, o) for m in range(N_CHIP) for o in range(N_CORE) if m or o]
+    others = [(m, o) for m in (7, 6, 5, 3, 4, 2, 1, 0) for o in range(N_CORE) if m or o]
     k_n = []
     for i, (m, o) in enumerate(others):
         k_n.append(rcopy(duown, duall.at[pl.ds(my_row, TOK)], ns.at[i], nr.at[i], peer(m), mate if o else core))
@@ -347,14 +349,15 @@
     vm = pltpu.VMEM
     dma = pltpu.SemaphoreType.DMA
     scratch = [
-        vm((D, HALF), BF16), vm((D, HALF), BF16), vm((D, WIN), BF16), vm((D, WIN), BF16),
+        vm((D, HALF), BF16), vm((D, HALF), BF16), vm((D, WIN + R * T), BF16), vm((D, WIN), BF16),
         vm((R, HALF), BF16), vm((R, WIN), BF16), vm((R, D), BF16), vm((T, C, D), BF16), vm((T, TOK), jnp.int32),
         vm((2 * TOK, D), BF16), vm((n_dev * TOK, D), BF16), vm((2 * TOK, HALF), BF16),
         vm((C * T, D), F32), vm((C * T, D), BF16), vm((C * T, D), BF16),
-        vm((WIN, R * T), BF16), vm((N_CHIP * TOK, R * T), BF16), vm((N_CHIP * TOK, WIN), F32),
+        vm((WIN, R * T), BF16), vm((R * T, WIN), BF16),
+        vm((N_CHIP * TOK, R * T), BF16), vm((N_CHIP * TOK, WIN), F32),
         vm((TOK, D), F32), vm((TOK, D), F32), vm((TOK, D), F32),
         vm((TOK, 128), BF16), vm((N_CHIP * TOK, 128), BF16),
-        vm((4, T * TOK, D), BF16), vm((4 * T * TOK, WIN), BF16), vm((4 * T * TOK, R * T), BF16),
+        vm((4, T * TOK, D), BF16), vm((N_CHIP * T * TOK, WIN), BF16), vm((N_CHIP * T * TOK, R * T), BF16),
         vm((N_CHIP, TOK, R * T), F32), vm((N_CHIP, TOK, R * T), F32),
         vm((TOK, R * T), BF16), vm((n_dev * TOK, R * T), BF16),
         vm((R * T, WIN), F32), vm((R * T, OWIN), F32),

time: 39.6 us -> 38.5 us (0.972)
  Pallas kernels: 38.7 us -> 37.5 us
    pallas_call x1, Pallas kernels: 38.1 us -> 36.9 us  [device_step(): call(tokens, labels, w_one, w_two.T, adapter_a.T, adapter_b, task_heads.t...]
where the time goes in v3:
time: 38.5 us; the launch traced here: 38.3 us
  Pallas kernels  37.5 us (97%)
  between operations  0.8 us (2%)
    pallas_call x1, Pallas kernels, device_step(): call(tokens, labels, w_one, w_two.T, adapter_a.T, adapter_b, task_heads.t...  36.9 us

profile of v3, /device:TPU:0, one launch (start us, length us, event | category | flops | bytes accessed | tf_op | source)
XLA Modules:
  0.0 38.3 jit_solution(9636093879371939931)
XLA Ops:
  0.6 36.9 %min_norm.1 = (f32[1,8]{1,0:T(1,128)S(1)}, f32[16,100]{1,0:T(8,128)S(1)}, f32[16,400]{1,0:T(8,128)S(1)}) custom-call(bf16[32,1600]{1,0:T(8,128)(2,1)} %x_hbm.1, s32[8,32]{1,0:T(8,128)} %lab_hbm.1, bf16[1600,6400]{1,0:T(8,128)(2,1)} %w1_hbm.1, bf16[1600,6400]{1,0:T(8,128)(2,1)} %bitcast.5, bf16[16,1600]{1,0:T(8,128)(2,1)} %bitcast.6, ...), custom_call_target="tpu_custom_call" | custom-call | tf_op jit(solution)/shard_map/min_norm/pallas_call | solution.py:392
  37.5 0.7 %put.1 = (f32[1,8]{1,0:T(1,128)}, f32[16,100]{1,0:T(8,128)}, f32[16,400]{1,0:T(8,128)}) custom-call(f32[1,8]{1,0:T(1,128)S(1)} %get-tuple-element.9.alpha_in, f32[16,100]{1,0:T(8,128)S(1)} %get-tuple-element.10.ga_in, f32[16,400]{1,0:T(8,128)S(1)} %get-tuple-element.11.gb_in), custom_call_target="tpu_custom_call" | custom-call | tf_op jit(solution)/shard_map/put/pallas_call | solution.py:395

commit v4 on v3

--- a/solution.py
+++ b/solution.py
@@ -20,9 +20,9 @@
 WIN = 896
 OWIN = 512
 W1_CHUNKS = ((0, 1536), (1536, 1664))
-W2_CHUNKS = ((0, 1024), (1024, 576))
+W2_CHUNKS = ((0, 512), (512, 512), (1024, 576))
 NEAR, FAR = (0, 1, 2, 4), (3, 5, 6, 7)
-BLOCKS = ((0,), (1, 2), (3, 5, 6, 7), (4,))
+BLOCKS = ((1, 2), (3, 5, 6, 7), (4,), (0,))
 GELU_C = 0.7978845608028654
 N_TILE = 256
 
@@ -142,7 +142,7 @@
     k_xp = rcopy(xp.at[pl.ds(0, TOK)], xp.at[pl.ds(TOK, TOK)], ps, pr, chip, mate)
     k_xp.start()
     k_x = {}
-    for m in (1, 2, 4, 3, 5, 6, 7):
+    for m in (1, 2, 4, 7):
         k_x[m] = rcopy(xp.at[pl.ds(0, TOK)], xall.at[pl.ds(my_row, TOK)], xs.at[m], xr.at[m], peer(m), core)
         k_x[m].start()
 
@@ -166,6 +166,16 @@
             pre = nn(x2, w1h[:, i:j]) + nn(u2, bmh[:, i:j])
             hbuf[:, i:j] = gelu(pre).astype(BF16)
     k_z = []
+    grp_row = pl.multiple_of(core * (N_CHIP * TOK), N_CHIP * TOK)
+
+    def relay():
+        for got in (1, 2, 4):
+            k_x[got].wait_recv()
+        for got, to in ((1, 2), (2, 4), (4, 1)):
+            rows = xall.at[pl.ds(pl.multiple_of(grp_row + peer(got) * TOK, TOK), TOK)]
+            k_x[got + to] = rcopy(rows, rows, xs.at[got + to], xr.at[got + to], peer(to), core)
+            k_x[got + to].start()
+
     for i, ((a, n), cp) in enumerate(zip(W2_CHUNKS, c_w2)):
         cp.wait()
         for j in range(a, a + n, N_TILE):
@@ -174,13 +184,14 @@
             zsend[:, j : min(j + N_TILE, a + n)] = z[TOK:]
         k_z.append(rcopy(zsend.at[:, pl.ds(a, n)], zrecv.at[:, pl.ds(a, n)], zs.at[i], zr.at[i], chip, mate))
         k_z[-1].start()
-
-    grp_row = pl.multiple_of(core * (N_CHIP * TOK), N_CHIP * TOK)
+        if i == 0:
+            relay()
+
     c_w1w.wait()
 
     def slopes(which, base):
         for m in which:
-            if m:
+            if m in FAR:
                 k_x[m].wait_recv()
         xc = jnp.concatenate(
             [xall[pl.ds(pl.multiple_of(grp_row + peer(m) * TOK, TOK), TOK), :] for m in which], axis=0
@@ -248,13 +259,12 @@
                 k_d[m].start()
         return dus
 
-    du_own = backward(BLOCKS[0])[0]
-    for block in BLOCKS[1:]:
-        if block == FAR:
-            slopes(FAR, len(NEAR) * TOK)
-            k_g = rcopy(xall.at[pl.ds(grp_row, N_CHIP * TOK)], xall.at[pl.ds(grp_row, N_CHIP * TOK)], gs, gr, chip, mate)
-            k_g.start()
+    slopes(FAR, len(NEAR) * TOK)
+    k_g = rcopy(xall.at[pl.ds(grp_row, N_CHIP * TOK)], xall.at[pl.ds(grp_row, N_CHIP * TOK)], gs, gr, chip, mate)
+    k_g.start()
+    for block in BLOCKS[:-1]:
         backward(block)
+    du_own = backward(BLOCKS[-1])[0]
     for a in range(0, WIN, N_TILE):
         gb[:, a : min(a + N_TILE, WIN)] = tn(ub[...], dp[:, a : min(a + N_TILE, WIN)])
 

time: 38.5 us -> 37.4 us (0.971)
  Pallas kernels: 37.5 us -> 36.5 us
    pallas_call x1, Pallas kernels: 36.9 us -> 35.9 us  [device_step(): call(tokens, labels, w_one, w_two.T, adapter_a.T, adapter_b, task_heads.t...]
where the time goes in v4:
time: 37.4 us; the launch traced here: 37.3 us
  Pallas kernels  36.5 us (98%)
  between operations  0.8 us (2%)
    pallas_call x1, Pallas kernels, device_step(): call(tokens, labels, w_one, w_two.T, adapter_a.T, adapter_b, task_heads.t...  35.9 us

profile of v4, /device:TPU:0, one launch (start us, length us, event | category | flops | bytes accessed | tf_op | source)
XLA Modules:
  0.0 37.3 jit_solution(8973784865432008052)
XLA Ops:
  0.6 35.9 %min_norm.1 = (f32[1,8]{1,0:T(1,128)S(1)}, f32[16,100]{1,0:T(8,128)S(1)}, f32[16,400]{1,0:T(8,128)S(1)}) custom-call(bf16[32,1600]{1,0:T(8,128)(2,1)} %x_hbm.1, s32[8,32]{1,0:T(8,128)} %lab_hbm.1, bf16[1600,6400]{1,0:T(8,128)(2,1)} %w1_hbm.1, bf16[1600,6400]{1,0:T(8,128)(2,1)} %bitcast.5, bf16[16,1600]{1,0:T(8,128)(2,1)} %bitcast.6, ...), custom_call_target="tpu_custom_call" | custom-call | tf_op jit(solution)/shard_map/min_norm/pallas_call | solution.py:402
  36.5 0.7 %put.1 = (f32[1,8]{1,0:T(1,128)}, f32[16,100]{1,0:T(8,128)}, f32[16,400]{1,0:T(8,128)}) custom-call(f32[1,8]{1,0:T(1,128)S(1)} %get-tuple-element.9.alpha_in, f32[16,100]{1,0:T(8,128)S(1)} %get-tuple-element.10.ga_in, f32[16,400]{1,0:T(8,128)S(1)} %get-tuple-element.11.gb_in), custom_call_target="tpu_custom_call" | custom-call | tf_op jit(solution)/shard_map/put/pallas_call | solution.py:405

commit v5 on v4

--- a/solution.py
+++ b/solution.py
@@ -144,7 +144,8 @@
     k_x = {}
     for m in (1, 2, 4, 7):
         k_x[m] = rcopy(xp.at[pl.ds(0, TOK)], xall.at[pl.ds(my_row, TOK)], xs.at[m], xr.at[m], peer(m), core)
-        k_x[m].start()
+        if m != 7:
+            k_x[m].start()
 
     c_at.wait()
     w1w[:, WIN:] = tn(at[...], row_of_r).astype(BF16)
@@ -165,6 +166,8 @@
             j = min(i + N_TILE, a + n)
             pre = nn(x2, w1h[:, i:j]) + nn(u2, bmh[:, i:j])
             hbuf[:, i:j] = gelu(pre).astype(BF16)
+        if a == 0:
+            k_x[7].start()
     k_z = []
     grp_row = pl.multiple_of(core * (N_CHIP * TOK), N_CHIP * TOK)
 

time: 37.4 us -> 36 us (0.963)
  Pallas kernels: 36.5 us -> 35.1 us
    pallas_call x1, Pallas kernels: 35.9 us -> 34.4 us  [device_step(): call(tokens, labels, w_one, w_two.T, adapter_a.T, adapter_b, task_heads.t...]
where the time goes in v5:
time: 36 us; the launch traced here: 35.9 us
  Pallas kernels  35.1 us (98%)
  between operations  0.8 us (2%)
    pallas_call x1, Pallas kernels, device_step(): call(tokens, labels, w_one, w_two.T, adapter_a.T, adapter_b, task_heads.t...  34.4 us

profile of v5, /device:TPU:0, one launch (start us, length us, event | category | flops | bytes accessed | tf_op | source)
XLA Modules:
  0.0 35.9 jit_solution(9987886626724392799)
XLA Ops:
  0.6 34.4 %min_norm.1 = (f32[1,8]{1,0:T(1,128)S(1)}, f32[16,100]{1,0:T(8,128)S(1)}, f32[16,400]{1,0:T(8,128)S(1)}) custom-call(bf16[32,1600]{1,0:T(8,128)(2,1)} %x_hbm.1, s32[8,32]{1,0:T(8,128)} %lab_hbm.1, bf16[1600,6400]{1,0:T(8,128)(2,1)} %w1_hbm.1, bf16[1600,6400]{1,0:T(8,128)(2,1)} %bitcast.5, bf16[16,1600]{1,0:T(8,128)(2,1)} %bitcast.6, ...), custom_call_target="tpu_custom_call" | custom-call | tf_op jit(solution)/shard_map/min_norm/pallas_call | solution.py:405
  35.1 0.7 %put.1 = (f32[1,8]{1,0:T(1,128)}, f32[16,100]{1,0:T(8,128)}, f32[16,400]{1,0:T(8,128)}) custom-call(f32[1,8]{1,0:T(1,128)S(1)} %get-tuple-element.9.alpha_in, f32[16,100]{1,0:T(8,128)S(1)} %get-tuple-element.10.ga_in, f32[16,400]{1,0:T(8,128)S(1)} %get-tuple-element.11.gb_in), custom_call_target="tpu_custom_call" | custom-call | tf_op jit(solution)/shard_map/put/pallas_call | solution.py:408

commit v6 on v5

--- a/solution.py
+++ b/solution.py
@@ -19,7 +19,7 @@
 OWN = BLK // N_CORE
 WIN = 896
 OWIN = 512
-W1_CHUNKS = ((0, 1536), (1536, 1664))
+W1_CHUNKS = ((0, 1024), (1024, 1024), (2048, 1152))
 W2_CHUNKS = ((0, 512), (512, 512), (1024, 576))
 NEAR, FAR = (0, 1, 2, 4), (3, 5, 6, 7)
 BLOCKS = ((1, 2), (3, 5, 6, 7), (4,), (0,))
@@ -166,7 +166,7 @@
             j = min(i + N_TILE, a + n)
             pre = nn(x2, w1h[:, i:j]) + nn(u2, bmh[:, i:j])
             hbuf[:, i:j] = gelu(pre).astype(BF16)
-        if a == 0:
+        if a == 1024:
             k_x[7].start()
     k_z = []
     grp_row = pl.multiple_of(core * (N_CHIP * TOK), N_CHIP * TOK)

time: 36 us -> 36.5 us (1.014)
  Pallas kernels: 35.1 us -> 35.5 us
    pallas_call x1, Pallas kernels: 34.4 us -> 34.9 us  [device_step(): call(tokens, labels, w_one, w_two.T, adapter_a.T, adapter_b, task_heads.t...]
where the time goes in v6:
time: 36.5 us; the launch traced here: 36.3 us
  Pallas kernels  35.5 us (97%)
  between operations  0.8 us (2%)
    pallas_call x1, Pallas kernels, device_step(): call(tokens, labels, w_one, w_two.T, adapter_a.T, adapter_b, task_heads.t...  34.9 us

profile of v6, /device:TPU:0, one launch (start us, length us, event | category | flops | bytes accessed | tf_op | source)
XLA Modules:
  0.0 36.3 jit_solution(14969531464709253203)
XLA Ops:
  0.6 34.9 %min_norm.1 = (f32[1,8]{1,0:T(1,128)S(1)}, f32[16,100]{1,0:T(8,128)S(1)}, f32[16,400]{1,0:T(8,128)S(1)}) custom-call(bf16[32,1600]{1,0:T(8,128)(2,1)} %x_hbm.1, s32[8,32]{1,0:T(8,128)} %lab_hbm.1, bf16[1600,6400]{1,0:T(8,128)(2,1)} %w1_hbm.1, bf16[1600,6400]{1,0:T(8,128)(2,1)} %bitcast.5, bf16[16,1600]{1,0:T(8,128)(2,1)} %bitcast.6, ...), custom_call_target="tpu_custom_call" | custom-call | tf_op jit(solution)/shard_map/min_norm/pallas_call | solution.py:405
  35.5 0.7 %put.1 = (f32[1,8]{1,0:T(1,128)}, f32[16,100]{1,0:T(8,128)}, f32[16,400]{1,0:T(8,128)}) custom-call(f32[1,8]{1,0:T(1,128)S(1)} %get-tuple-element.9.alpha_in, f32[16,100]{1,0:T(8,128)S(1)} %get-tuple-element.10.ga_in, f32[16,400]{1,0:T(8,128)S(1)} %get-tuple-element.11.gb_in), custom_call_target="tpu_custom_call" | custom-call | tf_op jit(solution)/shard_map/put/pallas_call | solution.py:408
